TPU v7x, 256 devices: a 4x2x16 block of a 4x16x16 slice. The times are simulated.
256 devices in a mesh: groups: 2 (over y), row: 16 (over z), col: 4 (over x), sub: 2 (over core).
Axes of the slice: x: 4, y: 2, z: 16, core: 2. Of those that a mesh axis runs over, the one named last changes fastest.
The devices are a block of a 4x16x16 slice.
Arguments:
- saved_alignment: bfloat16 [64, 1024, 256], P(('col', 'sub'), ('groups', 'row')), parts along dimension 1, may hold values from -6 to 6
- homolog_existence: int32 [64, 1024], P(('col', 'sub'), ('groups', 'row')), parts along dimension 1, may hold values 0 or 1
- amino_existence: int32 [1024], P(('groups', 'row')), parts along dimension 0, may hold values 0 or 1
- couple_delta_adjoint: bfloat16 [1024, 512, 128], P(('groups', 'row'), ('col', 'sub')), parts along dimension 0, may hold values from -1.5 to 1.5
- feedforward_adjoint: bfloat16 [64, 1024, 256], P(('col', 'sub'), ('groups', 'row')), parts along dimension 1, may hold values from -1.5 to 1.5
- feedforward_scale: float32 [256], replicated, may hold values from 0.1 to 1.9
- expansion_matrix: bfloat16 [256, 1024], replicated, may hold values from -0.375 to 0.375
- contraction_matrix: bfloat16 [1024, 256], replicated, may hold values from -0.1875 to 0.1875
- product_scale_vector: float32 [256], replicated, may hold values from 0.1 to 1.9
- twin_operand_matrix: bfloat16 [256, 64], replicated, may hold values from -0.375 to 0.375
- couple_projection_matrix: bfloat16 [1024, 128], replicated, may hold values from -0.1875 to 0.1875
Outputs:
- alignment_start_adjoint: bfloat16 [64, 1024, 256], P(('col', 'sub'), ('groups', 'row')), parts along dimension 1
- grad_out_weight: float32 [2048, 128], P('groups'), parts along dimension 0
- grad_factor_weight: float32 [512, 64], P('groups'), parts along dimension 0
- grad_w_in: float32 [512, 1024], P('groups'), parts along dimension 0
- grad_w_mid: float32 [2048, 256], P('groups'), parts along dimension 0
- feedforward_scale_adjoint: float32 [512], P('groups'), parts along dimension 0
- product_scale_adjoint: float32 [512], P('groups'), parts along dimension 0
There are 2 independent parts, one for each index of `groups`. A program takes and returns all parts, laid end to end along the dimension named above; an argument that names none is the same for every part. Nothing has to cross between parts.
All inputs are finite; a program needn't handle non-finite values. No bound on the sum of `homolog_existence` or of `amino_existence` on one device may be relied on, other than what follows from the above.
Results may differ from a plain program's by a relative error of at most 0.015.
Values may be sent and summed in bfloat16 or wider, within the bound.
No kernel may reach another device: no remote copies, remote signals or barrier semaphores. Data moves between devices by JAX's collectives and lax.ppermute only.
A program may use at most 64 MiB of HBM per device.

v0:
```python
import math
import jax
import jax.numpy as jnp
from jax import lax
from jax.sharding import PartitionSpec as P

epsilon = 1e-05


def in_one_piece(arrays, axis, dim, along):
    ends, at = ([], 0)
    for a in arrays[:-1]:
        at += a.shape[along]
        ends.append(at)
    both = jnp.concatenate(arrays, axis=along)
    return tuple(jnp.split(lax.all_gather(both, axis, axis=dim, tiled=True), ends, axis=along))


def joined_along(parts, dim):
    parts = jnp.moveaxis(parts, 0, dim)
    lengths = parts.shape
    return parts.reshape(*lengths[:dim], lengths[dim] * lengths[dim + 1], *lengths[dim + 2 :])


def one_gather(arrays, axis, dims):
    vector = jnp.concatenate([a.reshape(-1) for a in arrays])
    lines, at, done = (lax.all_gather(vector, axis), 0, [])
    for a, dim in zip(arrays, dims):
        parts = lines[:, at : at + a.size].reshape(-1, *a.shape)
        done.append(joined_along(parts, dim))
        at += a.size
    return tuple(done)


def split_up(shard, dim, devices):
    lengths = shard.shape
    parts = shard.reshape(*lengths[:dim], devices, lengths[dim] // devices, *lengths[dim + 1 :])
    return jnp.moveaxis(parts, dim, 0)


def sent_and_summed(shard, axis, dim):
    parts = split_up(shard, dim, lax.axis_size(axis))
    arrived = lax.all_to_all(parts, axis, split_axis=0, concat_axis=0, tiled=True)
    return arrived.astype(jnp.float32).sum(axis=0)


def layer_normalize(values):
    centre = jnp.mean(values, axis=-1, keepdims=True)
    centred = values - centre
    variance = jnp.mean(centred * centred, axis=-1, keepdims=True)
    inv_std = lax.rsqrt(variance + epsilon)
    return (centred * inv_std, inv_std)


def standardizer_adjoint(grad_hat, normed, inv_std):
    first_mean = jnp.mean(grad_hat, axis=-1, keepdims=True)
    second_mean = jnp.mean(grad_hat * normed, axis=-1, keepdims=True)
    return inv_std * (grad_hat - first_mean - normed * second_mean)


def exact_gelu(values):
    return jax.nn.gelu(values, approximate=False)


def contract_rows(first_arr, second_arr):
    return lax.dot_general(
        first_arr, second_arr, (((0,), (0,)), ((), ())), preferred_element_type=jnp.float32
    )


def contract_last(first_arr, second_arr):
    return lax.dot_general(
        first_arr, second_arr, (((1,), (1,)), ((), ())), preferred_element_type=jnp.float32
    )


def per_device(
    saved_alignment,
    homolog_existence,
    amino_existence,
    couple_delta_adjoint,
    feedforward_adjoint,
    feedforward_scale,
    expansion_matrix,
    contraction_matrix,
    product_scale_vector,
    twin_operand_matrix,
    couple_projection_matrix,
):
    homolog_split_total, amino_split_total, lane_breadth = saved_alignment.shape
    factor = twin_operand_matrix.shape[1] // 2
    pair_width = couple_projection_matrix.shape[1]
    existing_record_lines = homolog_split_total * amino_split_total
    shard_count = lax.axis_size(("col", "sub"))
    row_devices = lax.axis_size("row")
    total_res = amino_split_total * row_devices
    col_res = total_res // shard_count
    all_seqs = homolog_split_total * shard_count
    embedding_numbers = saved_alignment.astype(jnp.float32).reshape(
        existing_record_lines, lane_breadth
    )
    transition_standardized, transition_inv_deviation = layer_normalize(embedding_numbers)
    normalized_input = (transition_standardized * feedforward_scale).astype(jnp.bfloat16)
    hidden_pre = jnp.dot(normalized_input, expansion_matrix, preferred_element_type=jnp.float32)
    gelu_value, gelu_back = jax.vjp(exact_gelu, hidden_pre)
    hidden = gelu_value.astype(jnp.bfloat16)
    mixed_values = embedding_numbers + jnp.dot(
        hidden, contraction_matrix, preferred_element_type=jnp.float32
    )
    product_zscored, product_reciprocal_spread = layer_normalize(mixed_values)
    normalized_output = (product_zscored * product_scale_vector).astype(jnp.bfloat16)
    projected = jnp.dot(normalized_output, twin_operand_matrix, preferred_element_type=jnp.float32)
    keep_mask = (homolog_existence * amino_existence[None, :]).astype(jnp.float32)
    keep_col = keep_mask.reshape(existing_record_lines, 1)
    left_factor = (
        (projected[:, :factor] * keep_col)
        .astype(jnp.bfloat16)
        .reshape(homolog_split_total, amino_split_total * factor)
    )
    right_factor = (
        (projected[:, factor:] * keep_col)
        .astype(jnp.bfloat16)
        .reshape(homolog_split_total, amino_split_total * factor)
    )
    keep_half = keep_mask.astype(jnp.bfloat16)
    left_all, keep_rows = in_one_piece((left_factor, keep_half), ("col", "sub"), 0, 1)
    right_spread, keep_spread = one_gather((right_factor, keep_half), "row", (1, 1))
    right_flat, keep_cols = (
        lax.all_to_all(right_spread, ("col", "sub"), split_axis=1, concat_axis=0, tiled=True),
        lax.all_to_all(keep_spread, ("col", "sub"), split_axis=1, concat_axis=0, tiled=True),
    )
    right_cols = right_flat.reshape(all_seqs, col_res, factor)
    left_rows = left_all.reshape(all_seqs, amino_split_total, factor)
    pair_count = contract_rows(keep_rows, keep_cols)
    inverse = 1.0 / jnp.maximum(pair_count, 1.0)
    block_rows = math.gcd(amino_split_total, 16)
    result_adjoint = jnp.zeros((factor * factor, pair_width), jnp.float32)
    grad_right = jnp.zeros((all_seqs, col_res, factor), jnp.float32)
    left_parts = []
    for row_start in range(0, amino_split_total, block_rows):
        left_block = left_rows[:, row_start : row_start + block_rows, :]
        inv_block = inverse[row_start : row_start + block_rows]
        cot_block = couple_delta_adjoint[row_start : row_start + block_rows]
        outer_sum = jnp.einsum(
            "sip,sjq->ijpq", left_block, right_cols, preferred_element_type=jnp.float32
        )
        outer_half = (outer_sum * inv_block[:, :, None, None]).astype(jnp.bfloat16)
        outer_half = outer_half.reshape(block_rows, col_res, factor * factor)
        result_adjoint = result_adjoint + jnp.einsum(
            "ijk,ijl->kl", outer_half, cot_block, preferred_element_type=jnp.float32
        )
        pair_back = jnp.einsum(
            "ijl,kl->ijk", cot_block, couple_projection_matrix, preferred_element_type=jnp.float32
        )
        back_half = (pair_back * inv_block[:, :, None]).astype(jnp.bfloat16)
        back_half = back_half.reshape(block_rows, col_res, factor, factor)
        left_parts.append(
            jnp.einsum("ijpq,sjq->sip", back_half, right_cols, preferred_element_type=jnp.float32)
        )
        grad_right = grad_right + jnp.einsum(
            "ijpq,sip->sjq", back_half, left_block, preferred_element_type=jnp.float32
        )
    grad_left = jnp.concatenate(left_parts, axis=1).reshape(all_seqs, amino_split_total * factor)
    left_own = sent_and_summed(grad_left.astype(jnp.bfloat16), ("col", "sub"), 0)
    right_back = lax.all_to_all(
        grad_right.reshape(all_seqs, col_res * factor).astype(jnp.bfloat16),
        ("col", "sub"),
        split_axis=0,
        concat_axis=1,
        tiled=True,
    )
    right_own = sent_and_summed(right_back, "row", 1)
    grad_proj = jnp.concatenate(
        [
            left_own.reshape(existing_record_lines, factor),
            right_own.reshape(existing_record_lines, factor),
        ],
        axis=1,
    )
    grad_proj = (grad_proj * keep_col).astype(jnp.bfloat16)
    operand_adjoint = contract_rows(normalized_output, grad_proj)
    rescaled_result_adjoint = contract_last(grad_proj, twin_operand_matrix)
    product_scale_adjoint = jnp.sum(rescaled_result_adjoint * product_zscored, axis=0)
    combined_adjoint = feedforward_adjoint.astype(jnp.float32).reshape(
        existing_record_lines, lane_breadth
    ) + standardizer_adjoint(
        rescaled_result_adjoint * product_scale_vector, product_zscored, product_reciprocal_spread
    )
    grad_mixed_half = combined_adjoint.astype(jnp.bfloat16)
    hidden_adjoint = contract_rows(hidden, grad_mixed_half)
    grad_hidden = contract_last(grad_mixed_half, contraction_matrix)
    grad_pre = gelu_back(grad_hidden)[0].astype(jnp.bfloat16)
    expansion_adjoint = contract_rows(normalized_input, grad_pre)
    normed_input_gradient = contract_last(grad_pre, expansion_matrix)
    feedforward_scale_adjoint = jnp.sum(normed_input_gradient * transition_standardized, axis=0)
    alignment_start_adjoint = combined_adjoint + standardizer_adjoint(
        normed_input_gradient * feedforward_scale, transition_standardized, transition_inv_deviation
    )
    weight_grads = lax.psum(
        (
            result_adjoint,
            operand_adjoint,
            expansion_adjoint,
            hidden_adjoint,
            feedforward_scale_adjoint,
            product_scale_adjoint,
        ),
        ("row", "col", "sub"),
    )
    return (
        alignment_start_adjoint.astype(jnp.bfloat16).reshape(
            homolog_split_total, amino_split_total, lane_breadth
        ),
        weight_grads[0],
        weight_grads[1],
        weight_grads[2],
        weight_grads[3],
        weight_grads[4],
        weight_grads[5],
    )


def solution(mesh):
    return jax.shard_map(
        per_device,
        mesh=mesh,
        in_specs=(
            P(("col", "sub"), ("groups", "row"), None),
            P(("col", "sub"), ("groups", "row")),
            P(("groups", "row")),
            P(("groups", "row"), ("col", "sub"), None),
            P(("col", "sub"), ("groups", "row"), None),
            P(),
            P(),
            P(),
            P(),
            P(),
            P(),
        ),
        out_specs=(
            P(("col", "sub"), ("groups", "row"), None),
            P("groups", None),
            P("groups", None),
            P("groups", None),
            P("groups", None),
            P("groups"),
            P("groups"),
        ),
        check_vma=False,
    )
```

profile of v0, /device:TPU:33, one launch (start us, length us, event | category | flops | bytes accessed | tf_op | source)
XLA Modules:
  0.0 527.1 jit_solution(18394093957308587515)
XLA Ops:
  11.5 3.4 multiply_convert_fusion.2
  17.4 45.3 %all-gather.1 = bf16[16,1,8448]{2,1,0:T(2,128)(2,1)S(1)} all-gather(bf16[1,1,8448]{2,1,0:T(2,128)(2,1)S(1)} %reshape.176), channel_id=2, replica_groups=mesh['groups'=2,'row'=16,'col'=4,'sub'=2] {'row'}, dimensions={0}, use_global_device_ids=true | all-gather | bytes 287232 | tf_op jit(solution)/shard_map/all_gather | solution.py:27
  63.6 12.2 %all-to-all-start.1 = ((bf16[8,2,256]{2,1,0:T(2,128)(2,1)}), bf16[8,2,256]{2,1,0:T(2,128)(2,1)S(1)}, u32[]{:S(2)}, u32[]{:S(2)}) async-start(bf16[8,2,256]{2,1,0:T(2,128)(2,1)} %reshape.192), calls=%async_computation.1 | async-start | bytes 16384 | tf_op jit(solution)/shard_map/all_to_all | solution.py:130
  76.1 13.7 %all_gather.11 = bf16[64,1056]{1,0:T(8,128)(2,1)S(1)} all-gather(bf16[8,1056]{1,0:T(8,128)(2,1)S(1)} %pad_maximum_fusion.2), channel_id=1, replica_groups=mesh['groups'=2,'row'=16,'col'=4,'sub'=2] {'col','sub'}, dimensions={0}, use_global_device_ids=true | all-gather | bytes 152064 | tf_op jit(solution)/shard_map/all_gather | solution.py:16
  90.9 4.1 all-to-all-start
  95.3 1.7 multiply_convert_fusion
  97.1 3.2 copy.56
  100.3 1.7 multiply_convert_fusion.1
  102.0 3.2 copy.53
  105.2 3.8 fusion.10
  109.0 1.5 fusion.19
  111.2 1.8 convert_element_type.80
  113.1 5.0 all-to-all-start.3
  118.1 1.9 reshape.161
  120.9 3.6 fusion.29
  124.6 1.3 fusion.32
  128.9 4.8 all-to-all-start.2
  133.7 3.2 fusion.1
  139.0 4.0 all-to-all-start.4
  145.4 2.7 copy.67
  148.2 2.7 copy.70
  151.9 1.8 fusion.22
  153.8 2.7 all-to-all-done.4
  158.2 1.3 fusion.50
  159.6 2.1 add_convert_fusion
  161.7 1.3 fusion.67
  163.6 252.7 %all-reduce = (f32[256]{0:T(256)}, f32[256]{0:T(256)}) all-reduce(f32[256]{0:T(256)S(1)} %get-tuple-element.9, f32[256]{0:T(256)S(1)} %get-tuple-element.7), channel_id=1, replica_groups=mesh['groups'=2,'row'=16,'col'=4,'sub'=2] {'row','col','sub'}, use_global_device_ids=true, to_apply=%region_15.0 | all-reduce | flops 512 | bytes 4096 | tf_op jit(solution)/shard_map/psum | solution.py:199
  417.1 95.3 %all-reduce.4.cloned.1.call-done = (f32[1024,128]{1,0:T(8,128)}, f32[256,64]{0,1:T(8,128)}, f32[256,1024]{1,0:T(8,128)}, f32[1024,256]{1,0:T(8,128)}) async-done(((f32[1024,128]{1,0:T(8,128)}, f32[256,64]{0,1:T(8,128)}, f32[256,1024]{1,0:T(8,128)}, f32[1024,256]{1,0:T(8,128)}), (f32[1024,128]{1,0:T(8,128)}, f32[256,64]{0,1:T(8,128)}, f32[256,1024]{1,0:T(8,128)}, ...) | async-done | bytes 2686992 | tf_op jit(solution)/shard_map/psum | solution.py:199
  512.4 1.9 copy.122
  514.2 1.5 copy.123
  515.7 2.3 copy.124
  518.0 2.3 copy.125
  (122 shorter events, 22.6 us)
Async XLA Ops:
  7.2 4.3 copy-start
  8.4 6.6 %copy-start.17 = (f32[256]{0:T(256)}, f32[256]{0:T(256)S(1)}, u32[]{:S(2)}) copy-start(f32[256]{0:T(256)S(1)} %div.30) | copy-start | bytes 3076
  9.5 5.4 %copy-start.19 = (f32[256]{0:T(256)}, f32[256]{0:T(256)S(1)}, u32[]{:S(2)}) copy-start(f32[256]{0:T(256)S(1)} %rsqrt.20) | copy-start | bytes 3076
  10.3 6.7 %copy-start.21 = (f32[256]{0:T(256)}, f32[256]{0:T(256)S(1)}, u32[]{:S(2)}) copy-start(f32[256]{0:T(256)S(1)} %mul.200) | copy-start | bytes 3076
  11.5 4.3 copy-start.4
  11.5 4.3 copy-start.8
  11.5 5.3 copy-start.23
  11.5 5.4 %copy-start.10 = (bf16[256,64]{0,1:T(8,128)(2,1)S(1)}, bf16[256,64]{0,1:T(8,128)(2,1)}, u32[]{:S(2)}) copy-start(bf16[256,64]{0,1:T(8,128)(2,1)} %param.20) | copy-start | bytes 98308
  15.0 0.8 copy-start.5
  16.2 0.6 copy-start.13
  16.8 59.3 %copy-start.15 = (f32[256]{0:T(256)}, f32[256]{0:T(256)S(1)}, u32[]{:S(2)}) copy-start(f32[256]{0:T(256)S(1)} %add_rsqrt_fusion.1) | copy-start | bytes 3076
  63.6 27.3 %all-to-all-start.1 = ((bf16[8,2,256]{2,1,0:T(2,128)(2,1)}), bf16[8,2,256]{2,1,0:T(2,128)(2,1)S(1)}, u32[]{:S(2)}, u32[]{:S(2)}) async-start(bf16[8,2,256]{2,1,0:T(2,128)(2,1)} %reshape.192), calls=%async_computation.1 | async-start | bytes 16384 | tf_op jit(solution)/shard_map/all_to_all | solution.py:130
  90.9 22.1 %all-to-all-start = ((bf16[8,8,2048]{2,0,1:T(8,128)(2,1)}), bf16[8,8,2048]{2,0,1:T(8,128)(2,1)}, u32[]{:S(2)}, u32[]{:S(2)}) async-start(bf16[8,8,2048]{2,0,1:T(8,128)(2,1)} %copy.49), calls=%async_computation | async-start | bytes 524288 | tf_op jit(solution)/shard_map/all_to_all | solution.py:129
  105.2 3.8 copy-start.1
  113.1 15.9 %all-to-all-start.3 = ((bf16[8,8,2048]{2,1,0:T(8,128)(2,1)}), bf16[8,8,2048]{2,1,0:T(8,128)(2,1)S(1)}, u32[]{:S(2)}, u32[]{:S(2)}) async-start(bf16[8,8,2048]{2,1,0:T(8,128)(2,1)} %convert_element_type.80), calls=%async_computation.3 | async-start | bytes 524288 | tf_op jit(solution)/shard_map/all_to_all | solution.py:165
  120.9 3.7 copy-start.2
  128.9 10.1 %all-to-all-start.2 = ((bf16[8,8,1024]{2,1,0:T(8,128)(2,1)}), bf16[8,8,1024]{2,1,0:T(8,128)(2,1)S(1)}, u32[]{:S(2)}, u32[]{:S(2)}) async-start(bf16[8,8,1024]{2,1,0:T(8,128)(2,1)} %convert_element_type.77), calls=%async_computation.2 | async-start | bytes 262144 | tf_op jit(solution)/shard_map/all_to_all | solution.py:43
  139.0 17.5 %all-to-all-start.4 = ((bf16[16,8,1024]{2,1,0:T(8,128)(2,1)}), bf16[16,8,1024]{2,1,0:T(8,128)(2,1)S(1)}, u32[]{:S(2)}, u32[]{:S(2)}) async-start(bf16[16,8,1024]{2,1,0:T(8,128)(2,1)} %copy.65), calls=%async_computation.4 | async-start | bytes 524288 | tf_op jit(solution)/shard_map/all_to_all | solution.py:43
  143.0 369.4 %all-reduce.4.cloned.1.call-start = ((), (), s32[]{:S(2)}) async-start(), calls=%async_computation.5 | async-start | bytes 5373952 | tf_op jit(solution)/shard_map/psum | solution.py:199
  143.3 2.2 copy-start.3
  148.1 2.7 copy-start.7
  151.8 4.8 copy-start.22
  151.8 5.8 %copy-start.11 = (bf16[256,64]{0,1:T(8,128)(2,1)S(1)}, bf16[256,64]{0,1:T(8,128)(2,1)}, u32[]{:S(2)}) copy-start(bf16[256,64]{0,1:T(8,128)(2,1)} %param.20) | copy-start | bytes 98308
  151.8 5.8 %copy-start.14 = (f32[256]{0:T(256)S(1)}, f32[256]{0:T(256)}, u32[]{:S(2)}) copy-start(f32[256]{0:T(256)} %copy-done.13) | copy-start | bytes 3076
  151.8 5.8 %copy-start.16 = (f32[256]{0:T(256)S(1)}, f32[256]{0:T(256)}, u32[]{:S(2)}) copy-start(f32[256]{0:T(256)} %copy-done.15) | copy-start | bytes 3076
  151.9 5.8 %copy-start.24 = (f32[256]{0:T(256)S(1)}, f32[256]{0:T(256)}, u32[]{:S(2)}) copy-start(f32[256]{0:T(256)} %param.19) | copy-start | bytes 3076
  151.9 6.1 %copy-start.12 = (bf16[8,32,256]{2,1,0:T(8,128)(2,1)S(1)}, bf16[8,32,256]{2,1,0:T(8,128)(2,1)}, u32[]{:S(2)}) copy-start(bf16[8,32,256]{2,1,0:T(8,128)(2,1)} %param.15) | copy-start | bytes 393220
  151.9 6.3 %copy-start.6 = (bf16[256,1024]{1,0:T(8,128)(2,1)S(1)}, bf16[256,1024]{1,0:T(8,128)(2,1)}, u32[]{:S(2)}) copy-start(bf16[256,1024]{1,0:T(8,128)(2,1)} %copy-done.5) | copy-start | bytes 1572868
  151.9 7.7 %copy-start.9 = (bf16[1024,256]{1,0:T(8,128)(2,1)S(1)}, bf16[1024,256]{1,0:T(8,128)(2,1)}, u32[]{:S(2)}) copy-start(bf16[1024,256]{1,0:T(8,128)(2,1)} %param.18) | copy-start | bytes 1572868
  159.5 3.5 copy-start.18
  159.5 3.5 copy-start.20
  159.5 3.5 copy-start.25
Sparse Core Ops, SparseCore 0:
  163.2 349.1 all-reduce.3
where the time goes:
time: 528 us; the launch traced here: 527 us
  blocking collectives  312 us (59%)
  waiting for transfers between devices  99 us (19%)
  local copies, waits for them, and re-layouts  34.5 us (7%)
  matrix products  31.3 us (6%)
  starting transfers between devices  30.4 us (6%)
  between operations  14.6 us (3%)
  other arithmetic  5.63 us (1%)
    psum x1, blocking collectives, per_device(): lax.psum((result_adjoint, operand_adjoint, expansion_adjoint, hidden_adjo...  253 us
    psum x1, waiting for transfers between devices, per_device(): lax.psum((result_adjoint, operand_adjoint, expansion_adjoint, hidden_adjo...  95.3 us
    all_gather x1, blocking collectives, one_gather(): lines, at, done = (lax.all_gather(vector, axis), 0, [])  45.3 us
    all_gather x1, blocking collectives, in_one_piece(): lax.all_gather(both, axis, axis=dim, tiled=True)  13.7 us
    all_to_all x1, starting transfers between devices, per_device(): lax.all_to_all(keep_spread, ('col', 'sub'), split_axis=1, concat_axis=0,...  12.2 us
    unnamed x60, local copies, waits for them, and re-layouts  11 us
  transfers between devices with their start and end apart: 6, of which 3 were waited for; matrix products, arithmetic and copies ran while one was open for 9% of the time, Pallas kernels for 0%

commit v1 on v0

--- a/solution.py
+++ b/solution.py
@@ -3,6 +3,7 @@
 import jax.numpy as jnp
 from jax import lax
 from jax.sharding import PartitionSpec as P
+from jax.lax import psum
 
 epsilon = 1e-05
 
@@ -196,17 +197,16 @@
     alignment_start_adjoint = combined_adjoint + standardizer_adjoint(
         normed_input_gradient * feedforward_scale, transition_standardized, transition_inv_deviation
     )
-    weight_grads = lax.psum(
-        (
-            result_adjoint,
-            operand_adjoint,
-            expansion_adjoint,
-            hidden_adjoint,
-            feedforward_scale_adjoint,
-            product_scale_adjoint,
-        ),
-        ("row", "col", "sub"),
-    )
+    weight_grads = (
+        result_adjoint,
+        operand_adjoint,
+        expansion_adjoint,
+        hidden_adjoint,
+        feedforward_scale_adjoint,
+        product_scale_adjoint,
+    )
+    for j0 in (("col", "sub"), "row"):
+        weight_grads = psum(weight_grads, j0)
     return (
         alignment_start_adjoint.astype(jnp.bfloat16).reshape(
             homolog_split_total, amino_split_total, lane_breadth

time: 528 us -> 406 us (0.77)
  the two profiles are of different devices: /device:TPU:33 before, /device:TPU:34 now
where the time goes in v1:
time: 406 us; the launch traced here: 405 us
  waiting for transfers between devices  184 us (45%)
  blocking collectives  110 us (27%)
  local copies, waits for them, and re-layouts  35.1 us (9%)
  matrix products  31.3 us (8%)
  starting transfers between devices  24 us (6%)
  between operations  14.6 us (4%)
  other arithmetic  5.63 us (1%)
    psum x2, waiting for transfers between devices, per_device(): weight_grads = psum(weight_grads, j0)  177 us
    all_gather x1, blocking collectives, one_gather(): lines, at, done = (lax.all_gather(vector, axis), 0, [])  51.4 us
    psum x2, blocking collectives, per_device(): weight_grads = psum(weight_grads, j0)  45.2 us
    all_gather x1, blocking collectives, in_one_piece(): lax.all_gather(both, axis, axis=dim, tiled=True)  12.9 us
    unnamed x60, local copies, waits for them, and re-layouts  11.6 us
    all_to_all x2, starting transfers between devices, sent_and_summed(): lax.all_to_all(parts, axis, split_axis=0, concat_axis=0, tiled=True)  8.79 us
  transfers between devices with their start and end apart: 7, of which 4 were waited for; matrix products, arithmetic and copies ran while one was open for 11% of the time, Pallas kernels for 0%

profile of v1, /device:TPU:34, one launch (start us, length us, event | category | flops | bytes accessed | tf_op | source)
XLA Modules:
  0.0 404.6 jit_solution(7563100260490882166)
XLA Ops:
  11.5 3.4 multiply_convert_fusion.2
  17.9 51.4 %all-gather.1 = bf16[16,1,8448]{2,1,0:T(2,128)(2,1)S(1)} all-gather(bf16[1,1,8448]{2,1,0:T(2,128)(2,1)S(1)} %reshape.176), channel_id=2, replica_groups=mesh['groups'=2,'row'=16,'col'=4,'sub'=2] {'row'}, dimensions={0}, use_global_device_ids=true | all-gather | bytes 287232 | tf_op jit(solution)/shard_map/all_gather | solution.py:28
  70.3 5.0 %all-to-all-start.1 = ((bf16[8,2,256]{2,1,0:T(2,128)(2,1)}), bf16[8,2,256]{2,1,0:T(2,128)(2,1)S(1)}, u32[]{:S(2)}, u32[]{:S(2)}) async-start(bf16[8,2,256]{2,1,0:T(2,128)(2,1)} %reshape.192), calls=%async_computation.1 | async-start | bytes 16384 | tf_op jit(solution)/shard_map/all_to_all | solution.py:131
  75.6 12.9 %all_gather.11 = bf16[64,1056]{1,0:T(8,128)(2,1)S(1)} all-gather(bf16[8,1056]{1,0:T(8,128)(2,1)S(1)} %pad_maximum_fusion.2), channel_id=1, replica_groups=mesh['groups'=2,'row'=16,'col'=4,'sub'=2] {'col','sub'}, dimensions={0}, use_global_device_ids=true | all-gather | bytes 152064 | tf_op jit(solution)/shard_map/all_gather | solution.py:17
  89.7 4.8 %all-to-all-start = ((bf16[8,8,2048]{2,0,1:T(8,128)(2,1)}), bf16[8,8,2048]{2,0,1:T(8,128)(2,1)}, u32[]{:S(2)}, u32[]{:S(2)}) async-start(bf16[8,8,2048]{2,0,1:T(8,128)(2,1)} %copy.49), calls=%async_computation | async-start | bytes 524288 | tf_op jit(solution)/shard_map/all_to_all | solution.py:130
  94.8 1.7 multiply_convert_fusion
  96.6 3.2 copy.56
  99.8 1.7 multiply_convert_fusion.1
  101.5 3.2 copy.53
  104.7 3.8 fusion.10
  108.5 1.5 fusion.19
  110.7 1.8 convert_element_type.80
  112.6 5.0 %all-to-all-start.3 = ((bf16[8,8,2048]{2,1,0:T(8,128)(2,1)}), bf16[8,8,2048]{2,1,0:T(8,128)(2,1)S(1)}, u32[]{:S(2)}, u32[]{:S(2)}) async-start(bf16[8,8,2048]{2,1,0:T(8,128)(2,1)} %convert_element_type.80), calls=%async_computation.3 | async-start | bytes 524288 | tf_op jit(solution)/shard_map/all_to_all | solution.py:166
  117.6 1.9 reshape.161
  120.5 3.6 fusion.29
  128.4 4.8 %all-to-all-start.2 = ((bf16[8,8,1024]{2,1,0:T(8,128)(2,1)}), bf16[8,8,1024]{2,1,0:T(8,128)(2,1)S(1)}, u32[]{:S(2)}, u32[]{:S(2)}) async-start(bf16[8,8,1024]{2,1,0:T(8,128)(2,1)} %convert_element_type.77), calls=%async_computation.2 | async-start | bytes 262144 | tf_op jit(solution)/shard_map/all_to_all | solution.py:44
  133.3 3.2 fusion.1
  137.9 4.0 all-to-all-start.4
  144.4 2.7 copy.67
  147.1 2.7 copy.70
  150.8 1.8 fusion.22
  152.7 6.9 %all-to-all-done.4 = bf16[16,8,1024]{2,1,0:T(8,128)(2,1)S(1)} async-done(((bf16[16,8,1024]{2,1,0:T(8,128)(2,1)}), bf16[16,8,1024]{2,1,0:T(8,128)(2,1)S(1)}, u32[]{:S(2)}, u32[]{:S(2)}) %all-to-all-start.4) | async-done | bytes 262176 | tf_op jit(solution)/shard_map/all_to_all | solution.py:44
  161.3 1.3 fusion.50
  162.6 2.1 add_convert_fusion
  166.2 73.5 %all-reduce.9.cloned.1.call-done = (f32[1024,128]{1,0:T(8,128)}, f32[256,64]{0,1:T(8,128)}, f32[256,1024]{1,0:T(8,128)}, f32[1024,256]{1,0:T(8,128)}) async-done(((f32[1024,128]{1,0:T(8,128)}, f32[256,64]{0,1:T(8,128)}, f32[256,1024]{1,0:T(8,128)}, f32[1024,256]{1,0:T(8,128)}), (f32[1024,128]{1,0:T(8,128)}, f32[256,64]{0,1:T(8,128)}, f32[256,1024]{1,0:T(8,128)}, ...) | async-done | bytes 2686992 | tf_op jit(solution)/shard_map/psum | solution.py:209
  240.3 13.5 %all-reduce.2 = (f32[256]{0:T(256)S(1)}, f32[256]{0:T(256)S(1)}) all-reduce(f32[256]{0:T(256)S(1)} %get-tuple-element.9, f32[256]{0:T(256)S(1)} %get-tuple-element.7), channel_id=1, replica_groups=mesh['groups'=2,'row'=16,'col'=4,'sub'=2] {'col','sub'}, use_global_device_ids=true, to_apply=%region_19.0 | all-reduce | flops 512 | bytes 4096 | tf_op jit(solution)/shard_map/psum | solution.py:209
  253.8 31.7 %all-reduce = (f32[256]{0:T(256)}, f32[256]{0:T(256)}) all-reduce(f32[256]{0:T(256)S(1)} %get-tuple-element.19, f32[256]{0:T(256)S(1)} %get-tuple-element.20), channel_id=1, replica_groups=mesh['groups'=2,'row'=16,'col'=4,'sub'=2] {'row'}, use_global_device_ids=true, to_apply=%region_20.0 | all-reduce | flops 512 | bytes 4096 | tf_op jit(solution)/shard_map/psum | solution.py:209
  286.4 103.5 %all-reduce.7.cloned.1.call-done = (f32[1024,128]{1,0:T(8,128)}, f32[256,64]{0,1:T(8,128)}, f32[256,1024]{1,0:T(8,128)}, f32[1024,256]{1,0:T(8,128)}) async-done(((f32[1024,128]{1,0:T(8,128)}, f32[256,64]{0,1:T(8,128)}, f32[256,1024]{1,0:T(8,128)}, f32[1024,256]{1,0:T(8,128)}), (f32[1024,128]{1,0:T(8,128)}, f32[256,64]{0,1:T(8,128)}, f32[256,1024]{1,0:T(8,128)}, ...) | async-done | bytes 2686992 | tf_op jit(solution)/shard_map/psum | solution.py:209
  389.9 1.9 copy.126
  391.8 1.5 copy.127
  393.2 2.3 copy.128
  395.5 2.3 copy.129
  (126 shorter events, 25.3 us)
Async XLA Ops:
  7.2 4.3 %copy-start = (bf16[256,1024]{1,0:T(8,128)(2,1)S(1)}, bf16[256,1024]{1,0:T(8,128)(2,1)}, u32[]{:S(2)}) copy-start(bf16[256,1024]{1,0:T(8,128)(2,1)} %param.17) | copy-start | bytes 1572868
  8.4 2.1 copy-start.17
  9.5 0.9 copy-start.19
  10.3 7.3 %copy-start.21 = (f32[256]{0:T(256)}, f32[256]{0:T(256)S(1)}, u32[]{:S(2)}) copy-start(f32[256]{0:T(256)S(1)} %mul.200) | copy-start | bytes 3076
  11.5 4.3 %copy-start.4 = (bf16[8,32,256]{2,1,0:T(8,128)(2,1)S(1)}, bf16[8,32,256]{2,1,0:T(8,128)(2,1)}, u32[]{:S(2)}) copy-start(bf16[8,32,256]{2,1,0:T(8,128)(2,1)} %param.11) | copy-start | bytes 393220
  11.5 4.3 %copy-start.8 = (bf16[1024,256]{1,0:T(8,128)(2,1)S(1)}, bf16[1024,256]{1,0:T(8,128)(2,1)}, u32[]{:S(2)}) copy-start(bf16[1024,256]{1,0:T(8,128)(2,1)} %param.18) | copy-start | bytes 1572868
  11.5 5.8 %copy-start.23 = (f32[256]{0:T(256)S(1)}, f32[256]{0:T(256)}, u32[]{:S(2)}) copy-start(f32[256]{0:T(256)} %param.19) | copy-start | bytes 3076
  11.5 5.9 %copy-start.10 = (bf16[256,64]{0,1:T(8,128)(2,1)S(1)}, bf16[256,64]{0,1:T(8,128)(2,1)}, u32[]{:S(2)}) copy-start(bf16[256,64]{0,1:T(8,128)(2,1)} %param.20) | copy-start | bytes 98308
  15.0 0.8 copy-start.5
  16.2 0.6 copy-start.13
  70.3 19.4 %all-to-all-start.1 = ((bf16[8,2,256]{2,1,0:T(2,128)(2,1)}), bf16[8,2,256]{2,1,0:T(2,128)(2,1)S(1)}, u32[]{:S(2)}, u32[]{:S(2)}) async-start(bf16[8,2,256]{2,1,0:T(2,128)(2,1)} %reshape.192), calls=%async_computation.1 | async-start | bytes 16384 | tf_op jit(solution)/shard_map/all_to_all | solution.py:131
  89.7 22.8 %all-to-all-start = ((bf16[8,8,2048]{2,0,1:T(8,128)(2,1)}), bf16[8,8,2048]{2,0,1:T(8,128)(2,1)}, u32[]{:S(2)}, u32[]{:S(2)}) async-start(bf16[8,8,2048]{2,0,1:T(8,128)(2,1)} %copy.49), calls=%async_computation | async-start | bytes 524288 | tf_op jit(solution)/shard_map/all_to_all | solution.py:130
  104.7 3.8 copy-start.1
  112.6 15.9 %all-to-all-start.3 = ((bf16[8,8,2048]{2,1,0:T(8,128)(2,1)}), bf16[8,8,2048]{2,1,0:T(8,128)(2,1)S(1)}, u32[]{:S(2)}, u32[]{:S(2)}) async-start(bf16[8,8,2048]{2,1,0:T(8,128)(2,1)} %convert_element_type.80), calls=%async_computation.3 | async-start | bytes 524288 | tf_op jit(solution)/shard_map/all_to_all | solution.py:166
  120.4 3.7 copy-start.2
  128.4 9.5 %all-to-all-start.2 = ((bf16[8,8,1024]{2,1,0:T(8,128)(2,1)}), bf16[8,8,1024]{2,1,0:T(8,128)(2,1)S(1)}, u32[]{:S(2)}, u32[]{:S(2)}) async-start(bf16[8,8,1024]{2,1,0:T(8,128)(2,1)} %convert_element_type.77), calls=%async_computation.2 | async-start | bytes 262144 | tf_op jit(solution)/shard_map/all_to_all | solution.py:44
  137.9 21.7 %all-to-all-start.4 = ((bf16[16,8,1024]{2,1,0:T(8,128)(2,1)}), bf16[16,8,1024]{2,1,0:T(8,128)(2,1)S(1)}, u32[]{:S(2)}, u32[]{:S(2)}) async-start(bf16[16,8,1024]{2,1,0:T(8,128)(2,1)} %copy.65), calls=%async_computation.4 | async-start | bytes 524288 | tf_op jit(solution)/shard_map/all_to_all | solution.py:44
  141.9 97.9 %all-reduce.9.cloned.1.call-start = ((), (), s32[]{:S(2)}) async-start(), calls=%async_computation.6 | async-start | bytes 5373952 | tf_op jit(solution)/shard_map/psum | solution.py:209
  142.2 2.2 copy-start.3
  147.1 2.7 copy-start.7
  150.7 9.0 %copy-start.22 = (f32[256]{0:T(256)S(1)}, f32[256]{0:T(256)}, u32[]{:S(2)}) copy-start(f32[256]{0:T(256)} %copy-done.21) | copy-start | bytes 3076
  150.7 10.0 %copy-start.11 = (bf16[256,64]{0,1:T(8,128)(2,1)S(1)}, bf16[256,64]{0,1:T(8,128)(2,1)}, u32[]{:S(2)}) copy-start(bf16[256,64]{0,1:T(8,128)(2,1)} %param.20) | copy-start | bytes 98308
  150.8 10.0 %copy-start.14 = (f32[256]{0:T(256)S(1)}, f32[256]{0:T(256)}, u32[]{:S(2)}) copy-start(f32[256]{0:T(256)} %copy-done.13) | copy-start | bytes 3076
  150.8 10.0 %copy-start.16 = (f32[256]{0:T(256)S(1)}, f32[256]{0:T(256)}, u32[]{:S(2)}) copy-start(f32[256]{0:T(256)} %copy-done.15) | copy-start | bytes 3076
  150.8 9.9 %copy-start.24 = (f32[256]{0:T(256)S(1)}, f32[256]{0:T(256)}, u32[]{:S(2)}) copy-start(f32[256]{0:T(256)} %param.19) | copy-start | bytes 3076
  150.8 10.3 %copy-start.12 = (bf16[8,32,256]{2,1,0:T(8,128)(2,1)S(1)}, bf16[8,32,256]{2,1,0:T(8,128)(2,1)}, u32[]{:S(2)}) copy-start(bf16[8,32,256]{2,1,0:T(8,128)(2,1)} %param.15) | copy-start | bytes 393220
  150.8 10.5 %copy-start.6 = (bf16[256,1024]{1,0:T(8,128)(2,1)S(1)}, bf16[256,1024]{1,0:T(8,128)(2,1)}, u32[]{:S(2)}) copy-start(bf16[256,1024]{1,0:T(8,128)(2,1)} %copy-done.5) | copy-start | bytes 1572868
  150.8 11.8 %copy-start.9 = (bf16[1024,256]{1,0:T(8,128)(2,1)S(1)}, bf16[1024,256]{1,0:T(8,128)(2,1)}, u32[]{:S(2)}) copy-start(bf16[1024,256]{1,0:T(8,128)(2,1)} %param.18) | copy-start | bytes 1572868
  164.8 75.1 %copy-start.18 = (f32[256]{0:T(256)S(1)}, f32[256]{0:T(256)}, u32[]{:S(2)}) copy-start(f32[256]{0:T(256)} %copy-done.17) | copy-start | bytes 3076
  164.8 75.1 %copy-start.20 = (f32[256]{0:T(256)S(1)}, f32[256]{0:T(256)}, u32[]{:S(2)}) copy-start(f32[256]{0:T(256)} %copy-done.19) | copy-start | bytes 3076
  164.8 75.1 %copy-start.25 = (f32[256]{0:T(256)S(1)}, f32[256]{0:T(256)}, u32[]{:S(2)}) copy-start(f32[256]{0:T(256)} %param.16) | copy-start | bytes 3076
  166.2 223.7 %all-reduce.7.cloned.1.call-start = ((), (), s32[]{:S(2)}) async-start(), calls=%async_computation.5 | async-start | bytes 5373952 | tf_op jit(solution)/shard_map/psum | solution.py:209
  (1 other events, 0.6 us)
Sparse Core Ops, SparseCore 0:
  166.3 73.4 all-reduce.8
  242.4 147.4 all-reduce.6
